TPU v7x, 32 devices: a whole 2x2x4 slice. The times are simulated.
32 devices in a mesh: clients: 8 (over y, x, core), shard: 4 (over z).
Axes of the slice: x: 2, y: 2, z: 4, core: 2. Of those that a mesh axis runs over, the one named last changes fastest.
Arguments:
- client_deltas: bfloat16 [64, 32, 3584], P(('clients', 'shard')), may hold values from -6 to 6
- variate_deltas: bfloat16 [64, 32, 3584], P(('clients', 'shard')), may hold values from -6 to 6
- params: float32 [32, 3584], P(('clients', 'shard')), may hold values from -1.5 to 1.5
- variate: float32 [32, 3584], P(('clients', 'shard')), may hold values from -1.5 to 1.5
- taking_part: int32 [64], P(('clients', 'shard')), may hold values from 0 to 1, as said below
- counts: int32 [64], P(('clients', 'shard')), may hold values from 32 to 285
Outputs:
- new_params: float32 [32, 3584], P(('clients', 'shard'))
- new_variate: float32 [32, 3584], P(('clients', 'shard'))
- client_params: bfloat16 [32, 3584], replicated
- client_variate: bfloat16 [32, 3584], replicated
Inputs may be any that keep to these rules, and one draw needn't show every extreme that they name: `taking_part`: at least one client takes part.
All inputs are finite; a program needn't handle non-finite values.
Results may differ from a plain program's by a relative error of at most 0.001.
Values may be sent and summed in bfloat16 or wider, within the bound.
A program may use at most 64 MiB of HBM per device.

v0:
```python
import jax
import jax.numpy as jnp
from jax import lax
from jax.sharding import PartitionSpec as P


def weight_rows(taking_part, counts):
    weight = taking_part * counts
    upper_part = weight // 16 * 16
    lower_part = weight - upper_part
    weight_table = jnp.stack([upper_part, lower_part]).astype(jnp.bfloat16)
    chosen = taking_part.astype(jnp.bfloat16)[None, :]
    return (weight_table, chosen, jnp.sum(weight).astype(jnp.float32))


def weigh_blocks(weight_table, chosen, deltas, changes):
    client_count = deltas.shape[0]
    local_rows = deltas.shape[1]
    columns = deltas.shape[2]
    moved_sum = jnp.dot(
        weight_table, deltas.reshape(client_count, -1), preferred_element_type=jnp.float32
    )
    varied = jnp.dot(chosen, changes.reshape(client_count, -1), preferred_element_type=jnp.float32)
    return ((moved_sum[0] + moved_sum[1]).reshape(local_rows, columns), varied)


def body(client_deltas, variate_deltas, params, variate, taking_part, counts):
    all_part, all_counts = (
        lax.all_gather(taking_part, ("clients", "shard"), axis=0, tiled=True),
        lax.all_gather(counts, ("clients", "shard"), axis=0, tiled=True),
    )
    weight_table, chosen, weight_total = weight_rows(all_part, all_counts)
    client_count = all_part.shape[0]
    summed, shifted = weigh_blocks(
        weight_table,
        chosen,
        lax.all_to_all(
            client_deltas, ("clients", "shard"), split_axis=1, concat_axis=0, tiled=True
        ),
        lax.all_to_all(
            variate_deltas, ("clients", "shard"), split_axis=1, concat_axis=0, tiled=True
        ),
    )
    new_params = params + summed / weight_total
    new_variate = variate + shifted / jnp.float32(client_count)
    client_params, client_variate = (
        lax.all_gather(new_params.astype(jnp.bfloat16), ("clients", "shard"), axis=0, tiled=True),
        lax.all_gather(new_variate.astype(jnp.bfloat16), ("clients", "shard"), axis=0, tiled=True),
    )
    return (new_params, new_variate, client_params, client_variate)


def solution(mesh):
    in_specs = (
        P(("clients", "shard"), None, None),
        P(("clients", "shard"), None, None),
        P(("clients", "shard"), None),
        P(("clients", "shard"), None),
        P(("clients", "shard")),
        P(("clients", "shard")),
    )
    out_specs = (P(("clients", "shard"), None), P(("clients", "shard"), None), P(), P())
    return jax.shard_map(body, mesh=mesh, in_specs=in_specs, out_specs=out_specs, check_vma=False)
```

profile of v0, /device:TPU:0, one launch (start us, length us, event | category | flops | bytes accessed | tf_op | source)
XLA Modules:
  0.0 211.8 jit_solution(14549116178163955121)
XLA Ops:
  0.6 2.3 %copy.14 = bf16[2,32,3584]{2,0,1:T(2,128)(2,1)} copy(bf16[2,32,3584]{2,1,0:T(8,128)(2,1)} %param.6) | data formatting | bytes 917504 | tf_op args[0]
  2.9 0.0 copy-start
  2.9 7.3 %all-to-all-start = ((bf16[2,32,3584]{2,0,1:T(2,128)(2,1)}), bf16[2,32,3584]{2,0,1:T(2,128)(2,1)S(1)}, u32[]{:S(2)}, u32[]{:S(2)}) async-start(bf16[2,32,3584]{2,0,1:T(2,128)(2,1)} %copy.14), calls=%async_computation | async-start | bytes 917504 | tf_op jit(solution)/shard_map/all_to_all | solution.py:37
  10.2 0.0 copy-done
  10.2 1.2 copy.15
  11.5 11.7 %all-to-all-done = bf16[2,32,3584]{2,0,1:T(2,128)(2,1)S(1)} async-done(((bf16[2,32,3584]{2,0,1:T(2,128)(2,1)}), bf16[2,32,3584]{2,0,1:T(2,128)(2,1)S(1)}, u32[]{:S(2)}, u32[]{:S(2)}) %all-to-all-start) | async-done | bytes 458784 | tf_op jit(solution)/shard_map/all_to_all | solution.py:37
  23.2 4.1 %all-to-all-start.1 = ((bf16[2,32,3584]{2,0,1:T(2,128)(2,1)}), bf16[2,32,3584]{2,0,1:T(2,128)(2,1)S(1)}, u32[]{:S(2)}, u32[]{:S(2)}) async-start(bf16[2,32,3584]{2,0,1:T(2,128)(2,1)} %copy.15), calls=%async_computation.1 | async-start | bytes 917504 | tf_op jit(solution)/shard_map/all_to_all | solution.py:40
  27.3 0.0 copy-start.3
  27.3 0.6 copy-done.3
  27.9 0.2 dynamic-update-slice
  28.1 0.0 copy-start.4
  28.1 0.7 copy-done.4
  28.8 0.2 dynamic-update-slice.1
  28.9 40.4 %all-reduce.2 = (s32[64]{0:T(128)S(1)}, s32[64]{0:T(128)S(1)}) all-reduce(s32[64]{0:T(128)S(1)} %dynamic-update-slice, s32[64]{0:T(128)S(1)} %dynamic-update-slice.1), channel_id=1, replica_groups=mesh['clients'=8,'shard'=4] {'clients','shard'}, use_global_device_ids=true, to_apply=%add | all-reduce | flops 128 | bytes 1024
  69.4 0.6 convert_bitcast_fusion.2
  70.7 0.2 reshape.22
  70.9 0.0 all-to-all-done.1
  70.9 0.2 reshape.23
  71.1 0.2 convolution_reduce_fusion
  71.3 0.0 copy-start.1
  71.3 0.2 fusion
  71.4 0.5 copy-done.1
  72.0 0.6 convert_bitcast_fusion.1
  72.6 70.0 %all-gather = bf16[32,1,3584]{2,1,0:T(2,128)(2,1)S(1)} all-gather(bf16[1,1,3584]{2,1,0:T(2,128)(2,1)S(1)} %get-tuple-element.8), channel_id=1, replica_groups=mesh['clients'=8,'shard'=4] {'clients','shard'}, dimensions={0}, use_global_device_ids=true | all-gather | bytes 236544 | tf_op jit(solution)/shard_map/all_gather | solution.py:47
  142.6 0.0 copy-start.2
  142.6 0.7 copy.21
  143.3 0.0 copy-done.2
  143.3 0.6 convert_bitcast_fusion
  143.9 67.2 %all-gather.1 = bf16[32,1,3584]{2,1,0:T(2,128)(2,1)S(1)} all-gather(bf16[1,1,3584]{2,1,0:T(2,128)(2,1)S(1)} %get-tuple-element.6), channel_id=1, replica_groups=mesh['clients'=8,'shard'=4] {'clients','shard'}, dimensions={0}, use_global_device_ids=true | all-gather | bytes 236544 | tf_op jit(solution)/shard_map/all_gather | solution.py:48
  211.1 0.7 copy.20
  (4 shorter events, 0.0 us)
Async XLA Ops:
  2.9 7.3 %copy-start = (bf16[2,32,3584]{2,1,0:T(8,128)(2,1)S(1)}, bf16[2,32,3584]{2,1,0:T(8,128)(2,1)}, u32[]{:S(2)}) copy-start(bf16[2,32,3584]{2,1,0:T(8,128)(2,1)} %param.7) | copy-start | bytes 1376260
  2.9 20.3 %all-to-all-start = ((bf16[2,32,3584]{2,0,1:T(2,128)(2,1)}), bf16[2,32,3584]{2,0,1:T(2,128)(2,1)S(1)}, u32[]{:S(2)}, u32[]{:S(2)}) async-start(bf16[2,32,3584]{2,0,1:T(2,128)(2,1)} %copy.14), calls=%async_computation | async-start | bytes 917504 | tf_op jit(solution)/shard_map/all_to_all | solution.py:37
  23.2 47.7 %all-to-all-start.1 = ((bf16[2,32,3584]{2,0,1:T(2,128)(2,1)}), bf16[2,32,3584]{2,0,1:T(2,128)(2,1)S(1)}, u32[]{:S(2)}, u32[]{:S(2)}) async-start(bf16[2,32,3584]{2,0,1:T(2,128)(2,1)} %copy.15), calls=%async_computation.1 | async-start | bytes 917504 | tf_op jit(solution)/shard_map/all_to_all | solution.py:40
  27.3 0.7 copy-start.3
  28.1 0.7 copy-start.4
  71.3 0.7 copy-start.1
  142.6 0.7 copy-start.2
where the time goes:
time: 213 us; the launch traced here: 212 us
  blocking collectives  178 us (84%)
  waiting for transfers between devices  11.7 us (5%)
  starting transfers between devices  11.4 us (5%)
  local copies, waits for them, and re-layouts  7.49 us (4%)
    all_gather x1, blocking collectives, body(): lax.all_gather(new_params.astype(jnp.bfloat16), ('clients', 'shard'), axi...  70 us
    all_gather x1, blocking collectives, body(): lax.all_gather(new_variate.astype(jnp.bfloat16), ('clients', 'shard'), ax...  67.2 us
    unnamed x1, blocking collectives  40.4 us
    all_to_all x1, waiting for transfers between devices, body(): lax.all_to_all(client_deltas, ('clients', 'shard'), split_axis=1, concat_...  11.7 us
    all_to_all x1, starting transfers between devices, body(): lax.all_to_all(client_deltas, ('clients', 'shard'), split_axis=1, concat_...  7.33 us
    unnamed x18, local copies, waits for them, and re-layouts  7.14 us
  transfers between devices with their start and end apart: 2, of which 1 were waited for; matrix products, arithmetic and copies ran while one was open for 1% of the time, Pallas kernels for 0%

commit v1 on v0

--- a/solution.py
+++ b/solution.py
@@ -34,8 +34,14 @@
     summed, shifted = weigh_blocks(
         weight_table,
         chosen,
-        lax.all_to_all(
-            client_deltas, ("clients", "shard"), split_axis=1, concat_axis=0, tiled=True
+        jnp.concatenate(
+            lax.all_to_all(
+                jnp.stack(jnp.split(client_deltas, lax.axis_size(("clients", "shard")), axis=1)),
+                ("clients", "shard"),
+                0,
+                0,
+            ),
+            axis=0,
         ),
         lax.all_to_all(
             variate_deltas, ("clients", "shard"), split_axis=1, concat_axis=0, tiled=True

time: 213 us -> 227 us (1.066)
  local copies, waits for them, and re-layouts: 7.49 us -> 28 us
  waiting for transfers between devices: 11.7 us -> 0.01 us
  blocking collectives: 178 us -> 182 us
    unnamed x18 -> x50, local copies, waits for them, and re-layouts: 7.14 us -> 24.6 us
    all_to_all x1, waiting for transfers between devices: 11.7 us -> 0.01 us  [body(): lax.all_to_all(jnp.stack(jnp.split(client_deltas, lax.axis_size(('clients...]
    all_gather x1, blocking collectives: 70 us -> 73.4 us  [body(): lax.all_gather(new_params.astype(jnp.bfloat16), ('clients', 'shard'), axi...]
    split x0 -> x2, local copies, waits for them, and re-layouts: none -> 2.5 us  [body(): jnp.split(client_deltas, lax.axis_size(('clients', 'shard')), axis=1)]
  transfers between devices with their start and end apart: 2 -> 2, of which waited for: 1 -> 0; matrix products, arithmetic and copies ran while one was open for 1% -> 2% of each run, Pallas kernels for 0% -> 0%
where the time goes in v1:
time: 227 us; the launch traced here: 226 us
  blocking collectives  182 us (80%)
  local copies, waits for them, and re-layouts  28 us (12%)
  starting transfers between devices  12 us (5%)
    all_gather x1, blocking collectives, body(): lax.all_gather(new_params.astype(jnp.bfloat16), ('clients', 'shard'), axi...  73.4 us
    all_gather x1, blocking collectives, body(): lax.all_gather(new_variate.astype(jnp.bfloat16), ('clients', 'shard'), ax...  68.5 us
    unnamed x1, blocking collectives  40.4 us
    unnamed x50, local copies, waits for them, and re-layouts  24.6 us
    all_to_all x1, starting transfers between devices, body(): lax.all_to_all(jnp.stack(jnp.split(client_deltas, lax.axis_size(('clients...  7.33 us
    all_to_all x1, starting transfers between devices, body(): lax.all_to_all(variate_deltas, ('clients', 'shard'), split_axis=1, concat...  4.65 us
  transfers between devices with their start and end apart: 2, of which 0 were waited for; matrix products, arithmetic and copies ran while one was open for 2% of the time, Pallas kernels for 0%

profile of v1, /device:TPU:0, one launch (start us, length us, event | category | flops | bytes accessed | tf_op | source)
XLA Modules:
  0.0 226.0 jit_solution(6104810912641985082)
XLA Ops:
  0.6 2.1 fusion.10
  3.2 0.6 constant_dynamic-update-slice_fusion.31
  3.8 0.6 constant_dynamic-update-slice_fusion.30
  4.4 0.6 constant_dynamic-update-slice_fusion.29
  5.0 0.6 constant_dynamic-update-slice_fusion.28
  5.6 0.6 constant_dynamic-update-slice_fusion.27
  6.2 0.6 constant_dynamic-update-slice_fusion.26
  6.8 0.6 constant_dynamic-update-slice_fusion.25
  7.4 0.6 constant_dynamic-update-slice_fusion.24
  8.1 0.6 constant_dynamic-update-slice_fusion.23
  8.7 0.6 constant_dynamic-update-slice_fusion.22
  9.3 0.6 constant_dynamic-update-slice_fusion.21
  9.9 0.6 constant_dynamic-update-slice_fusion.20
  10.5 0.6 constant_dynamic-update-slice_fusion.19
  11.1 0.6 constant_dynamic-update-slice_fusion.18
  11.7 0.6 constant_dynamic-update-slice_fusion.17
  12.3 0.6 constant_dynamic-update-slice_fusion.16
  13.0 0.6 constant_dynamic-update-slice_fusion.15
  13.6 0.6 constant_dynamic-update-slice_fusion.14
  14.2 0.6 constant_dynamic-update-slice_fusion.13
  14.8 0.6 constant_dynamic-update-slice_fusion.12
  15.4 0.6 constant_dynamic-update-slice_fusion.11
  16.0 0.6 constant_dynamic-update-slice_fusion.10
  16.6 0.6 constant_dynamic-update-slice_fusion.9
  17.3 0.6 constant_dynamic-update-slice_fusion.8
  17.9 0.6 constant_dynamic-update-slice_fusion.7
  18.5 0.6 constant_dynamic-update-slice_fusion.6
  19.1 0.6 constant_dynamic-update-slice_fusion.5
  19.7 0.6 constant_dynamic-update-slice_fusion.4
  20.3 0.6 constant_dynamic-update-slice_fusion.3
  20.9 0.6 constant_dynamic-update-slice_fusion.2
  21.6 0.6 constant_dynamic-update-slice_fusion.1
  22.2 0.6 constant_dynamic-update-slice_fusion
  22.8 7.3 %all-to-all-start = ((bf16[32,2,1,3584]{3,1,2,0:T(2,128)(2,1)}), bf16[32,2,1,3584]{3,1,2,0:T(2,128)(2,1)S(1)}, u32[]{:S(2)}, u32[]{:S(2)}) async-start(bf16[32,2,1,3584]{3,1,2,0:T(2,128)(2,1)} %constant_dynamic-update-slice_fusion), calls=%async_computation | async-start | bytes 917504 | tf_op jit(solution)/shard_map/all_to_all | solution.py:38
  30.2 0.6 copy-done.4
  31.0 0.7 copy-done.5
  31.8 40.4 %all-reduce.2 = (s32[64]{0:T(128)S(1)}, s32[64]{0:T(128)S(1)}) all-reduce(s32[64]{0:T(128)S(1)} %dynamic-update-slice, s32[64]{0:T(128)S(1)} %dynamic-update-slice.1), channel_id=1, replica_groups=mesh['clients'=8,'shard'=4] {'clients','shard'}, use_global_device_ids=true, to_apply=%add | all-reduce | flops 128 | bytes 1024
  72.3 0.6 convert_bitcast_fusion.2
  73.6 1.2 copy.136
  74.8 4.7 %all-to-all-start.1 = ((bf16[2,32,3584]{2,0,1:T(2,128)(2,1)}), bf16[2,32,3584]{2,0,1:T(2,128)(2,1)S(1)}, u32[]{:S(2)}, u32[]{:S(2)}) async-start(bf16[2,32,3584]{2,0,1:T(2,128)(2,1)} %copy.136), calls=%async_computation.1 | async-start | bytes 917504 | tf_op jit(solution)/shard_map/all_to_all | solution.py:46
  79.8 0.5 copy-done.2
  80.4 0.6 convert_bitcast_fusion.1
  81.0 73.4 %all-gather = bf16[32,1,3584]{2,1,0:T(2,128)(2,1)S(1)} all-gather(bf16[1,1,3584]{2,1,0:T(2,128)(2,1)S(1)} %get-tuple-element.8), channel_id=1, replica_groups=mesh['clients'=8,'shard'=4] {'clients','shard'}, dimensions={0}, use_global_device_ids=true | all-gather | bytes 236544 | tf_op jit(solution)/shard_map/all_gather | solution.py:53
  154.4 0.7 copy.268
  155.5 0.7 copy-done.3
  156.2 0.6 convert_bitcast_fusion
  156.8 68.5 %all-gather.1 = bf16[32,1,3584]{2,1,0:T(2,128)(2,1)S(1)} all-gather(bf16[1,1,3584]{2,1,0:T(2,128)(2,1)S(1)} %get-tuple-element.6), channel_id=1, replica_groups=mesh['clients'=8,'shard'=4] {'clients','shard'}, dimensions={0}, use_global_device_ids=true | all-gather | bytes 236544 | tf_op jit(solution)/shard_map/all_gather | solution.py:54
  225.3 0.7 copy.267
  (21 shorter events, 1.5 us)
Async XLA Ops:
  0.6 2.1 copy-start
  22.8 50.8 %copy-start.1 = (bf16[2,32,3584]{2,1,0:T(8,128)(2,1)S(1)}, bf16[2,32,3584]{2,1,0:T(8,128)(2,1)}, u32[]{:S(2)}) copy-start(bf16[2,32,3584]{2,1,0:T(8,128)(2,1)} %param.7) | copy-start | bytes 1376260
  22.8 52.0 %all-to-all-start = ((bf16[32,2,1,3584]{3,1,2,0:T(2,128)(2,1)}), bf16[32,2,1,3584]{3,1,2,0:T(2,128)(2,1)S(1)}, u32[]{:S(2)}, u32[]{:S(2)}) async-start(bf16[32,2,1,3584]{3,1,2,0:T(2,128)(2,1)} %constant_dynamic-update-slice_fusion), calls=%async_computation | async-start | bytes 917504 | tf_op jit(solution)/shard_map/all_to_all | solution.py:38
  30.1 0.7 copy-start.4
  31.0 0.7 copy-start.5
  74.8 80.3 %all-to-all-start.1 = ((bf16[2,32,3584]{2,0,1:T(2,128)(2,1)}), bf16[2,32,3584]{2,0,1:T(2,128)(2,1)S(1)}, u32[]{:S(2)}, u32[]{:S(2)}) async-start(bf16[2,32,3584]{2,0,1:T(2,128)(2,1)} %copy.136), calls=%async_computation.1 | async-start | bytes 917504 | tf_op jit(solution)/shard_map/all_to_all | solution.py:46
  79.7 0.7 copy-start.2
  155.4 0.7 copy-start.3
